TPU v7x, 32 devices: a whole 2x2x4 slice. The times are simulated.
32 devices in a mesh: dp: 8 (over z, y), ep: 4 (over x, core).
Axes of the slice: x: 2, y: 2, z: 4, core: 2. Of those that a mesh axis runs over, the one named last changes fastest.
Arguments:
- tokens: bfloat16 [128, 4096], P(('dp', 'ep')), may hold values from -6 to 6
- router: float32 [4096, 8], replicated, may hold values from -0.1875 to 0.1875
- expert_ids: int32 [128, 2], P(('dp', 'ep')), may hold values from 0 to 7, all different within a row; in each aligned block of 4 rows (0 to 3, 4 to 7, ...) at most 2 rows name the same one
- w_gate: bfloat16 [8, 4096, 12288], P('dp', None, 'ep'), may hold values from -0.09375 to 0.09375
- w_up: bfloat16 [8, 4096, 12288], P('dp', None, 'ep'), may hold values from -0.09375 to 0.09375
- w_down: bfloat16 [8, 12288, 4096], P('dp', 'ep'), may hold values from -0.0546875 to 0.0546875
- states: bfloat16 [128, 16, 8192], P('dp', None, 'ep'), may hold values from -6 to 6
- kv_blocks: bfloat16 [256, 2, 16, 1024], P('dp', None, None, 'ep'), may hold values from -6 to 6
- plan_slots: int32 [8, 2, 3], replicated, may hold values from -1 to 15, as said below
- plan_len: int32 [8, 2], replicated, may hold values from 0 to 32, as said below
- plan_blocks: int32 [8, 2, 2, 2], replicated, may hold values from -1 to 31, as said below
Outputs:
- mixed: bfloat16 [128, 4096], P(('dp', 'ep'))
- new_states: bfloat16 [128, 16, 8192], P('dp', None, 'ep')
- new_cache: bfloat16 [256, 2, 16, 1024], P('dp', None, None, 'ep')
Inputs may be any that keep to these rules, and one draw needn't show every extreme that they name: `expert_ids`: in the rows of one device no expert is named more than 2 times. `plan_slots`: A move is live exactly where its first entry is not -1, and then all three entries are set; otherwise all are -1. For each m there is one distance d_m from 1 to 7, distinct for distinct m, such that every live move (r, m) goes to rank (r + d_m) mod 8. The leaving slots of a rank are distinct, the slots taken at a rank are distinct and differ from its leaving slots. Some rank has all 2 moves live. `plan_len`: zero exactly where the move is not live; some move holds 32 tokens. `plan_blocks`: entry j of both tables is -1 exactly where j * 16 >= plan_len. The blocks leaving a rank are distinct, the blocks taken at a rank are distinct and differ from the ones leaving it.
All inputs are finite; a program needn't handle non-finite values.
Results may differ from a plain program's by a relative error of at most 0.005.
Values may be sent and summed in bfloat16 or wider, within the bound.
A program may use at most 128 MiB of HBM per device.

v0:
```python
import jax
import jax.numpy as jnp
from jax import lax
from jax.sharding import PartitionSpec as P

CAP = 2


def local(
    tokens,
    router,
    expert_ids,
    w_gate,
    w_up,
    w_down,
    states,
    kv_blocks,
    plan_slots,
    plan_len,
    plan_blocks,
):
    ranks = lax.axis_size("dp")
    here = lax.axis_index("dp")
    moves = plan_slots.shape[1]
    slot_count = states.shape[0]
    block_count = kv_blocks.shape[0]
    per_request = plan_blocks.shape[3]
    block_len = kv_blocks.shape[2]
    mine = lax.dynamic_index_in_dim(plan_slots, here, 0, keepdims=False)
    my_blocks = lax.dynamic_index_in_dim(plan_blocks, here, 0, keepdims=False)
    my_length = lax.dynamic_index_in_dim(plan_len, here, 0, keepdims=False)
    leaving_slot = mine[:, 0]
    leaving_block = my_blocks[:, 0, :]
    state_out = states[jnp.maximum(leaving_slot, 0)]
    state_out = jnp.where((leaving_slot >= 0)[:, None, None], state_out, jnp.zeros_like(state_out))
    cache_out = kv_blocks[jnp.maximum(leaving_block, 0)]
    position = jnp.arange(per_request)[:, None] * block_len + jnp.arange(block_len)[None, :]
    written = (leaving_block >= 0)[:, :, None] & (position[None] < my_length[:, None, None])
    cache_out = jnp.where(written[:, :, None, :, None], cache_out, jnp.zeros_like(cache_out))
    arrivals = plan_slots[:, :, 1] == here
    sender = jnp.sum(jnp.where(arrivals, jnp.arange(ranks)[:, None], 0), axis=0)
    arriving = jnp.any(arrivals, axis=0)
    peers = jnp.arange(ranks)
    match = mine[:, 1][None, :] == peers[:, None]
    which = jnp.sum(jnp.where(match, jnp.arange(moves)[None, :], 0), axis=1)
    filled = jnp.any(match, axis=1)
    send_state = jnp.where(
        filled[:, None, None], state_out[which], jnp.zeros_like(state_out[which])
    )
    send_cache = jnp.where(
        filled[:, None, None, None, None], cache_out[which], jnp.zeros_like(cache_out[which])
    )
    got_state, got_cache = (
        lax.all_to_all(send_state, "dp", split_axis=0, concat_axis=0, tiled=True),
        lax.all_to_all(send_cache, "dp", split_axis=0, concat_axis=0, tiled=True),
    )
    state_in = got_state[sender]
    cache_in = got_cache[sender]
    slot_line = jnp.arange(slot_count)
    gone = jnp.any(slot_line[:, None] == leaving_slot[None, :], axis=1)
    new_states = jnp.where(gone[:, None, None], jnp.zeros_like(states), states)
    block_line = jnp.arange(block_count)
    gone_blocks = jnp.any(block_line[:, None, None] == leaving_block[None], axis=(1, 2))
    new_cache = jnp.where(gone_blocks[:, None, None, None], jnp.zeros_like(kv_blocks), kv_blocks)
    for move_index in range(moves):
        anchor = sender[move_index]
        place = plan_slots[anchor, move_index, 2]
        landing = (slot_line == place) & arriving[move_index]
        new_states = jnp.where(landing[:, None, None], state_in[move_index][None], new_states)
        for block_index in range(per_request):
            spot = plan_blocks[anchor, move_index, 1, block_index]
            block_hit = (block_line == spot) & arriving[move_index]
            new_cache = jnp.where(
                block_hit[:, None, None, None], cache_in[move_index, block_index][None], new_cache
            )
    experts = router.shape[1]
    tok_count = tokens.shape[0]
    width = tokens.shape[1]
    group = ranks // experts
    flat_ids = expert_ids.reshape(-1)
    onehot = (flat_ids[:, None] == jnp.arange(experts)[None, :]).astype(jnp.int32)
    earlier = jnp.cumsum(onehot, axis=0) - onehot
    slot_of = jnp.sum(earlier * onehot, axis=1)
    target_row = flat_ids * CAP + slot_of
    placer = (jnp.arange(experts * CAP)[:, None] == target_row[None, :]).astype(jnp.bfloat16)
    doubled = jnp.repeat(tokens, 2, axis=0)
    packed = jnp.dot(placer, doubled, preferred_element_type=jnp.float32).astype(jnp.bfloat16)
    outgoing = jnp.repeat(packed.reshape(experts, CAP, width), group, axis=0)
    incoming = lax.all_to_all(outgoing, "dp", split_axis=0, concat_axis=0, tiled=True)
    rows_in = incoming.reshape(ranks * CAP, width)
    piece = lax.all_gather(rows_in, "ep", axis=0, tiled=True)
    gate = jnp.dot(piece, w_gate[0], preferred_element_type=jnp.float32)
    upper = jnp.dot(piece, w_up[0], preferred_element_type=jnp.float32)
    hidden = (jax.nn.silu(gate) * upper).astype(jnp.bfloat16)
    summed = lax.psum_scatter(
        jnp.dot(hidden, w_down[0], preferred_element_type=jnp.float32),
        "ep",
        scatter_dimension=0,
        tiled=True,
    )
    returned = lax.all_to_all(
        summed.reshape(ranks, CAP, width), "dp", split_axis=0, concat_axis=0, tiled=True
    )
    expert_out = jnp.sum(returned.reshape(experts, group, CAP, width), axis=1).reshape(
        experts * CAP, width
    )
    chosen = expert_out[target_row].reshape(tok_count, 2, width)
    logits = jnp.dot(tokens.astype(jnp.float32), router, precision=lax.Precision.HIGHEST)
    scores = jax.nn.sigmoid(jnp.take_along_axis(logits, expert_ids, axis=1))
    weights = scores / jnp.sum(scores, axis=1, keepdims=True)
    mixed = jnp.sum(weights[:, :, None] * chosen, axis=1).astype(jnp.bfloat16)
    return (mixed, new_states, new_cache)


def solution(mesh):
    placed = (
        P(("dp", "ep"), None),
        P(),
        P(("dp", "ep"), None),
        P("dp", None, "ep"),
        P("dp", None, "ep"),
        P("dp", "ep", None),
        P("dp", None, "ep"),
        P("dp", None, None, "ep"),
        P(),
        P(),
        P(),
    )
    return jax.shard_map(
        local,
        mesh=mesh,
        in_specs=placed,
        out_specs=(P(("dp", "ep"), None), P("dp", None, "ep"), P("dp", None, None, "ep")),
        check_vma=False,
    )
```

profile of v0, /device:TPU:0, one launch (start us, length us, event | category | flops | bytes accessed | tf_op | source)
XLA Modules:
  0.0 140.0 jit_solution(5067093591805837852)
XLA Ops:
  10.1 7.3 %all-to-all-start = ((bf16[8,2,4096]{2,1,0:T(2,128)(2,1)}), bf16[8,2,4096]{2,1,0:T(2,128)(2,1)S(1)}, u32[]{:S(2)}, u32[]{:S(2)}) async-start(bf16[8,2,4096]{2,1,0:T(2,128)(2,1)} %reshape_broadcast_in_dim_reshape.3), calls=%async_computation | async-start | bytes 262144 | tf_op jit(solution)/shard_map/all_to_all | solution.py:89
  23.4 0.9 dynamic-slice_reduce_fusion
  25.7 1.4 %constant_dynamic-slice_fusion.7 = (s32[1,1,1]{0,1,2:T(1,128)}, s32[1,1,1]{0,1,2:T(1,128)}) fusion(s32[8,2,3]{0,1,2:T(2,128)} %param.19, s32[]{:T(128)S(6)} %select_n.118, s32[]{:T(128)S(6)} %select_n.125), kind=kLoop, calls=%fused_computation.72 | loop fusion | bytes 24 | tf_op jit(solution)/shard_map/dynamic_slice | solution.py:67
  27.1 1.4 constant_dynamic-slice_fusion.6
  30.8 1.8 %compare_and_fusion.5 = pred[16]{0:T(512)(128)(4,1)} fusion(pred[]{:T(512)} %bitcast.17, s32[]{:T(128)} %bitcast.16), kind=kLoop, calls=%fused_computation.63 | loop fusion | flops 32 | bytes 21 | tf_op jit(solution)/shard_map/and | solution.py:68
  32.5 1.8 %compare_and_fusion.1 = pred[32]{0:T(512)(128)(4,1)} fusion(pred[]{:T(512)} %bitcast.17, s32[]{:T(128)} %bitcast.27), kind=kLoop, calls=%fused_computation.58 | loop fusion | flops 64 | bytes 37 | tf_op jit(solution)/shard_map/and | solution.py:72
  34.3 1.8 %compare_and_fusion.2 = pred[32]{0:T(512)(128)(4,1)} fusion(pred[]{:T(512)} %bitcast.17, s32[]{:T(128)} %bitcast.25), kind=kLoop, calls=%fused_computation.59 | loop fusion | flops 64 | bytes 37 | tf_op jit(solution)/shard_map/and | solution.py:72
  37.1 1.8 %gather_fusion.1 = bf16[2,16,2048]{2,1,0:T(8,128)(2,1)S(1)} fusion(bf16[16,16,2048]{2,1,0:T(8,128)(2,1)} %param.17, s32[1024]{0:T(1024)S(1)} %pad_clamp_fusion.3), kind=kCustom, calls=%fused_computation.1 | custom fusion | bytes 262152 | tf_op jit(solution)/shard_map/gather | solution.py:34
  39.0 1.6 %gather_fusion.4 = bf16[4,2,16,256]{3,2,1,0:T(8,128)(2,1)S(1)} fusion(bf16[32,2,16,256]{3,2,1,0:T(8,128)(2,1)} %param.18, s32[1024]{0:T(1024)S(1)} %pad_clamp_fusion), kind=kCustom, calls=%fused_computation.4 | custom fusion | bytes 131088 | tf_op jit(solution)/shard_map/gather | solution.py:36
  42.1 1.8 %compare_and_fusion.6 = pred[16]{0:T(512)(128)(4,1)} fusion(pred[]{:T(512)} %bitcast.9, s32[]{:T(128)} %bitcast.8), kind=kLoop, calls=%fused_computation.64 | loop fusion | flops 32 | bytes 21 | tf_op jit(solution)/shard_map/and | solution.py:68
  43.9 1.0 fusion.32
  44.9 6.0 %all-to-all-start.3 = ((bf16[8,2,2,16,256]{4,3,2,1,0:T(8,128)(2,1)}), bf16[8,2,2,16,256]{4,3,2,1,0:T(8,128)(2,1)S(1)}, u32[]{:S(2)}, u32[]{:S(2)}) async-start(bf16[8,2,2,16,256]{4,3,2,1,0:T(8,128)(2,1)} %broadcast_select_fusion.1), calls=%async_computation.4 | async-start | bytes 524288 | tf_op jit(solution)/shard_map/all_to_all | solution.py:55
  51.0 7.2 %all_gather.3 = bf16[64,4096]{1,0:T(8,128)(2,1)S(1)} all-gather(bf16[16,4096]{1,0:T(8,128)(2,1)S(1)} %reshape.211), channel_id=1, replica_groups=mesh['dp'=8,'ep'=4] {'ep'}, dimensions={0}, use_global_device_ids=true | all-gather | bytes 655360 | tf_op jit(solution)/shard_map/all_gather | solution.py:91
  58.2 10.4 %fusion.4 = f32[64,3072]{1,0:T(8,128)S(1)} fusion(bf16[64,4096]{1,0:T(8,128)(2,1)S(1)} %all_gather.3, bf16[1,4096,3072]{2,1,0:T(8,128)(2,1)} %param.14), kind=kOutput, calls=%fused_computation.12 | convolution fusion | flops 1610612736 | bytes 26476544 | tf_op jit(solution)/shard_map/dot_general | solution.py:92
  68.7 20.9 %fusion = f32[64,4096]{1,0:T(8,128)} fusion(bf16[1,3072,4096]{2,1,0:T(8,128)(2,1)} %param.16, bf16[64,4096]{1,0:T(8,128)(2,1)S(1)} %all_gather.3, bf16[1,4096,3072]{2,1,0:T(8,128)(2,1)} %param.15, f32[64,3072]{1,0:T(8,128)S(1)} %fusion.4), kind=kOutput, calls=%fused_computation.8 | convolution fusion | flops 3222405120 | bytes 52690944 | tf_op jit(solution)/shard_map/dot_general | solution.py:96
  89.7 1.2 compare_and_fusion.3
  93.5 6.0 %all-to-all-start.2 = ((bf16[8,16,2048]{2,1,0:T(8,128)(2,1)}), bf16[8,16,2048]{2,1,0:T(8,128)(2,1)S(1)}, u32[]{:S(2)}, u32[]{:S(2)}) async-start(bf16[8,16,2048]{2,1,0:T(8,128)(2,1)} %broadcast_select_fusion), calls=%async_computation.3 | async-start | bytes 1048576 | tf_op jit(solution)/shard_map/all_to_all | solution.py:54
  99.5 1.3 compare_and_fusion.4
  101.5 1.7 %select_select_fusion.1 = bf16[32,2,16,256]{3,2,1,0:T(8,128)(2,1)} fusion(bf16[32,2,16,256]{3,2,1,0:T(8,128)(2,1)S(1)} %copy-done.3, pred[32]{0:T(512)(128)(4,1)S(1)} %compare_reduce_fusion, pred[32]{0:T(512)(128)(4,1)} %compare_and_fusion.1, pred[32]{0:T(512)(128)(4,1)} %compare_and_fusion.2, pred[32]{0:T(512)(128)(4,1)S(1)} %compare_and_fusion.3, ...), kind=kLoop, calls=%fused_computation.23 | loop fusion | flops 1310720 | bytes 1114272 | tf_op jit(solution)/shard_map/jit(_where)/select_n | solution.py:73
  103.2 11.3 %all-to-all-done.2 = bf16[8,16,2048]{2,1,0:T(8,128)(2,1)S(1)} async-done(((bf16[8,16,2048]{2,1,0:T(8,128)(2,1)}), bf16[8,16,2048]{2,1,0:T(8,128)(2,1)S(1)}, u32[]{:S(2)}, u32[]{:S(2)}) %all-to-all-start.2) | async-done | bytes 524320 | tf_op jit(solution)/shard_map/all_to_all | solution.py:54
  115.3 1.8 %reshape.212 = f32[8,2,4096]{2,1,0:T(2,128)} reshape(f32[16,4096]{1,0:T(8,128)} %reduce-scatter.2.cloned.1.call-done) | data formatting | bytes 524288 | tf_op jit(solution)/shard_map/reshape | solution.py:102
  117.1 5.5 %all-to-all-start.1 = ((f32[8,2,4096]{2,1,0:T(2,128)}), f32[8,2,4096]{2,1,0:T(2,128)S(1)}, u32[]{:S(2)}, u32[]{:S(2)}) async-start(f32[8,2,4096]{2,1,0:T(2,128)} %reshape.212), calls=%async_computation.2 | async-start | bytes 524288 | tf_op jit(solution)/shard_map/all_to_all | solution.py:101
  122.6 1.9 %select_select_fusion = bf16[16,16,2048]{2,1,0:T(8,128)(2,1)} fusion(bf16[16,16,2048]{2,1,0:T(8,128)(2,1)S(1)} %copy-done.2, pred[16]{0:T(512)(128)(4,1)S(1)} %compare_reduce_fusion.1, pred[16]{0:T(512)(128)(4,1)} %compare_and_fusion.5, pred[16]{0:T(512)(128)(4,1)} %compare_and_fusion.6, bf16[16,2048]{1,0:T(8,128)(2,1)S(1)} %get-tuple-element.7, ...), kind=kLoop, calls=%fused_computation.17 | loop fusion | flops 1572864 | bytes 2228272 | tf_op jit(solution)/shard_map/jit(_where)/select_n | solution.py:69
  124.5 6.8 %all-to-all-done.1 = f32[8,2,4096]{2,1,0:T(2,128)S(1)} async-done(((f32[8,2,4096]{2,1,0:T(2,128)}), f32[8,2,4096]{2,1,0:T(2,128)S(1)}, u32[]{:S(2)}, u32[]{:S(2)}) %all-to-all-start.1) | async-done | bytes 262176 | tf_op jit(solution)/shard_map/all_to_all | solution.py:101
  (89 shorter events, 17.3 us)
Async XLA Ops:
  7.2 36.8 %copy-start = (f32[4096,8]{0,1:T(8,128)S(1)}, f32[4096,8]{0,1:T(8,128)}, u32[]{:S(2)}) copy-start(f32[4096,8]{0,1:T(8,128)} %param.12) | copy-start | bytes 393220
  10.1 34.8 %all-to-all-start = ((bf16[8,2,4096]{2,1,0:T(2,128)(2,1)}), bf16[8,2,4096]{2,1,0:T(2,128)(2,1)S(1)}, u32[]{:S(2)}, u32[]{:S(2)}) async-start(bf16[8,2,4096]{2,1,0:T(2,128)(2,1)} %reshape_broadcast_in_dim_reshape.3), calls=%async_computation | async-start | bytes 262144 | tf_op jit(solution)/shard_map/all_to_all | solution.py:89
  19.3 16.9 %copy-start.9 = (s32[2]{0:T(128)}, s32[2]{0:T(128)S(1)}, u32[]{:S(2)}) copy-start(s32[2]{0:T(128)S(1)} %get-tuple-element.5) | copy-start | bytes 28
  23.4 34.8 %copy-start.5 = (pred[8]{0:T(512)(128)(4,1)}, pred[8]{0:T(512)(128)(4,1)S(1)}, u32[]{:S(2)}) copy-start(pred[8]{0:T(512)(128)(4,1)S(1)} %fusion.25) | copy-start | bytes 28
  30.8 5.5 %copy-start.7 = (s32[2,1,2]{2,1,0:T(1,128)}, s32[2,1,2]{2,1,0:T(1,128)S(1)}, u32[]{:S(2)}) copy-start(s32[2,1,2]{2,1,0:T(1,128)S(1)} %get-tuple-element.19) | copy-start | bytes 52
  44.9 48.7 %all-to-all-start.3 = ((bf16[8,2,2,16,256]{4,3,2,1,0:T(8,128)(2,1)}), bf16[8,2,2,16,256]{4,3,2,1,0:T(8,128)(2,1)S(1)}, u32[]{:S(2)}, u32[]{:S(2)}) async-start(bf16[8,2,2,16,256]{4,3,2,1,0:T(8,128)(2,1)} %broadcast_select_fusion.1), calls=%async_computation.4 | async-start | bytes 524288 | tf_op jit(solution)/shard_map/all_to_all | solution.py:55
  50.9 64.3 %reduce-scatter.2.cloned.1.call-start = ((), (), s32[]{:S(2)}) async-start(), calls=%async_computation.5 | async-start | bytes 1310720 | tf_op jit(solution)/shard_map/reduce_scatter | solution.py:95
  68.6 22.3 %copy-start.4 = (s32[4,2,1]{0,1,2:T(2,128)S(1)}, s32[4,2,1]{0,1,2:T(2,128)}, u32[]{:S(2)}) copy-start(s32[4,2,1]{0,1,2:T(2,128)} %bitcast_or_fusion) | copy-start | bytes 100
  68.6 23.9 %copy-start.10 = (s32[2]{0:T(128)S(1)}, s32[2]{0:T(128)}, u32[]{:S(2)}) copy-start(s32[2]{0:T(128)} %copy-done.9) | copy-start | bytes 28
  68.7 24.0 %copy-start.6 = (pred[8]{0:T(512)(128)(4,1)S(1)}, pred[8]{0:T(512)(128)(4,1)}, u32[]{:S(2)}) copy-start(pred[8]{0:T(512)(128)(4,1)} %copy-done.5) | copy-start | bytes 28
  68.7 32.1 %copy-start.8 = (s32[2,1,2]{2,1,0:T(1,128)S(1)}, s32[2,1,2]{2,1,0:T(1,128)}, u32[]{:S(2)}) copy-start(s32[2,1,2]{2,1,0:T(1,128)} %copy-done.7) | copy-start | bytes 52
  68.7 32.8 %copy-start.3 = (bf16[32,2,16,256]{3,2,1,0:T(8,128)(2,1)S(1)}, bf16[32,2,16,256]{3,2,1,0:T(8,128)(2,1)}, u32[]{:S(2)}) copy-start(bf16[32,2,16,256]{3,2,1,0:T(8,128)(2,1)} %param.18) | copy-start | bytes 1572868
  68.7 53.9 %copy-start.2 = (bf16[16,16,2048]{2,1,0:T(8,128)(2,1)S(1)}, bf16[16,16,2048]{2,1,0:T(8,128)(2,1)}, u32[]{:S(2)}) copy-start(bf16[16,16,2048]{2,1,0:T(8,128)(2,1)} %param.17) | copy-start | bytes 3145732
  68.7 64.5 %copy-start.1 = (f32[4096,8]{0,1:T(8,128)S(1)}, f32[4096,8]{0,1:T(8,128)}, u32[]{:S(2)}) copy-start(f32[4096,8]{0,1:T(8,128)} %param.12) | copy-start | bytes 393220
  93.5 21.0 %all-to-all-start.2 = ((bf16[8,16,2048]{2,1,0:T(8,128)(2,1)}), bf16[8,16,2048]{2,1,0:T(8,128)(2,1)S(1)}, u32[]{:S(2)}, u32[]{:S(2)}) async-start(bf16[8,16,2048]{2,1,0:T(8,128)(2,1)} %broadcast_select_fusion), calls=%async_computation.3 | async-start | bytes 1048576 | tf_op jit(solution)/shard_map/all_to_all | solution.py:54
  117.1 14.3 %all-to-all-start.1 = ((f32[8,2,4096]{2,1,0:T(2,128)}), f32[8,2,4096]{2,1,0:T(2,128)S(1)}, u32[]{:S(2)}, u32[]{:S(2)}) async-start(f32[8,2,4096]{2,1,0:T(2,128)} %reshape.212), calls=%async_computation.2 | async-start | bytes 524288 | tf_op jit(solution)/shard_map/all_to_all | solution.py:101
Sparse Core Ops, SparseCore 0:
  89.8 25.4 reduce-scatter.1
where the time goes:
time: 141 us; the launch traced here: 140 us
  matrix products  32.5 us (23%)
  starting transfers between devices  24.9 us (18%)
  other arithmetic  20.1 us (14%)
  local copies, waits for them, and re-layouts  18.9 us (13%)
  waiting for transfers between devices  18.3 us (13%)
  between operations  18.2 us (13%)
  blocking collectives  7.17 us (5%)
    dot_general x1, matrix products, local(): jnp.dot(hidden, w_down[0], preferred_element_type=jnp.float32)  20.9 us
    all_to_all x1, waiting for transfers between devices, local(): lax.all_to_all(send_state, 'dp', split_axis=0, concat_axis=0, tiled=True)  11.3 us
    dot_general x1, matrix products, local(): gate = jnp.dot(piece, w_gate[0], preferred_element_type=jnp.float32)  10.4 us
    all_to_all x1, starting transfers between devices, local(): lax.all_to_all(outgoing, 'dp', split_axis=0, concat_axis=0, tiled=True)  7.31 us
    all_gather x1, blocking collectives, local(): piece = lax.all_gather(rows_in, 'ep', axis=0, tiled=True)  7.17 us
    all_to_all x1, waiting for transfers between devices, local(): lax.all_to_all(summed.reshape(ranks, CAP, width), 'dp', split_axis=0, con...  6.8 us
    and x4, other arithmetic, local(): block_hit = (block_line == spot) & arriving[move_index]  6.06 us
    all_to_all x1, starting transfers between devices, local(): lax.all_to_all(send_cache, 'dp', split_axis=0, concat_axis=0, tiled=True)  6.04 us
  transfers between devices with their start and end apart: 5, of which 3 were waited for; matrix products, arithmetic and copies ran while one was open for 46% of the time, Pallas kernels for 0%

commit v1 on v0

--- a/solution.py
+++ b/solution.py
@@ -1,9 +1,413 @@
+import functools
+
 import jax
 import jax.numpy as jnp
 from jax import lax
+from jax.experimental import pallas as pl
+from jax.experimental.pallas import tpu as pltpu
 from jax.sharding import PartitionSpec as P
 
 CAP = 2
+MESH = pl.DeviceIdType.MESH
+ANY = pl.BlockSpec(memory_space=pl.ANY)
+VMEM = pl.BlockSpec(memory_space=pltpu.VMEM)
+SMEM = pl.BlockSpec(memory_space=pltpu.SMEM)
+VMEM_LIMIT = 67_000_000
+UP_TILE = 256
+DOWN_TILE = 512
+RING = 8
+
+
+def target_rows(ids_ref, tok_count):
+    picks = [ids_ref[t, k] for t in range(tok_count) for k in range(2)]
+    rows = []
+    for p, expert in enumerate(picks):
+        slot = jnp.int32(0)
+        for q in range(p):
+            slot = slot + jnp.where(picks[q] == expert, 1, 0)
+        rows.append(expert * CAP + slot)
+    return picks, rows
+
+
+def prepare_kernel(
+    ids_ref, slots_ref, len_ref, blocks_ref, tok_ref, states_ref, kv_ref,
+    packed_ref, send_state, send_cache, base_states, base_cache,
+    s_buf, c_buf, s_pay, c_pay, load_sem, pay_sem, cpay_sem, store_sem,
+):
+    here = lax.axis_index("dp")
+    moves = slots_ref.shape[1]
+    per_request = blocks_ref.shape[3]
+    block_len = kv_ref.shape[2]
+    load_s = pltpu.make_async_copy(states_ref, s_buf, load_sem.at[0])
+    load_c = pltpu.make_async_copy(kv_ref, c_buf, load_sem.at[1])
+    load_s.start()
+    load_c.start()
+    tok_count = tok_ref.shape[0]
+    experts = packed_ref.shape[0]
+    _, rows = target_rows(ids_ref, tok_count)
+    row_at = lax.broadcasted_iota(jnp.int32, (experts * CAP, tok_count), 0)
+    tok_at = lax.broadcasted_iota(jnp.int32, (experts * CAP, tok_count), 1)
+    placer = jnp.zeros((experts * CAP, tok_count), jnp.float32)
+    for p, row in enumerate(rows):
+        placer = jnp.where((row_at == row) & (tok_at == p // 2), 1.0, placer)
+    packed = jnp.dot(
+        placer.astype(jnp.bfloat16), tok_ref[...], preferred_element_type=jnp.float32
+    ).astype(jnp.bfloat16)
+    for e in range(experts):
+        packed_ref[e] = packed[e * CAP : (e + 1) * CAP]
+    load_s.wait()
+    load_c.wait()
+    for m in range(moves):
+        slot = slots_ref[here, m, 0]
+        dest = slots_ref[here, m, 1]
+
+        @pl.when(slot >= 0)
+        def _():
+            s_pay[m] = s_buf[slot]
+            s_buf[slot] = jnp.zeros_like(s_pay[m])
+            pltpu.make_async_copy(s_pay.at[m], send_state.at[dest], pay_sem.at[m]).start()
+
+        for j in range(per_request):
+            block = blocks_ref[here, m, 0, j]
+
+            @pl.when(block >= 0)
+            def _():
+                value = c_buf[block]
+                position = j * block_len + lax.broadcasted_iota(jnp.int32, value.shape, 1)
+                c_pay[m, j] = jnp.where(
+                    position < len_ref[here, m], value.astype(jnp.float32), 0.0
+                ).astype(value.dtype)
+                c_buf[block] = jnp.zeros_like(value)
+                pltpu.make_async_copy(
+                    c_pay.at[m, j], send_cache.at[dest, j], cpay_sem.at[m, j]
+                ).start()
+
+    store_s = pltpu.make_async_copy(s_buf, base_states, store_sem.at[0])
+    store_c = pltpu.make_async_copy(c_buf, base_cache, store_sem.at[1])
+    store_s.start()
+    store_c.start()
+    for m in range(moves):
+        slot = slots_ref[here, m, 0]
+        dest = slots_ref[here, m, 1]
+
+        @pl.when(slot >= 0)
+        def _():
+            pltpu.make_async_copy(s_pay.at[m], send_state.at[dest], pay_sem.at[m]).wait()
+
+        for j in range(per_request):
+
+            @pl.when(blocks_ref[here, m, 0, j] >= 0)
+            def _():
+                pltpu.make_async_copy(
+                    c_pay.at[m, j], send_cache.at[dest, j], cpay_sem.at[m, j]
+                ).wait()
+
+    store_s.wait()
+    store_c.wait()
+
+
+def land_kernel(
+    slots_ref, blocks_ref, got_state, got_cache, base_states, base_cache,
+    new_states, new_cache, s_buf, c_buf, in_s, in_c, out_s, out_c,
+):
+    here = lax.axis_index("dp")
+    ranks, moves = slots_ref.shape[0], slots_ref.shape[1]
+    per_request = blocks_ref.shape[3]
+    plan = []
+    for m in range(moves):
+        anchor, arriving = jnp.int32(0), jnp.int32(0)
+        for r in range(ranks):
+            hit = slots_ref[r, m, 1] == here
+            anchor = jnp.where(hit, r, anchor)
+            arriving = jnp.where(hit, 1, arriving)
+        lands = [
+            (arriving > 0) & (blocks_ref[anchor, m, 1, j] >= 0) for j in range(per_request)
+        ]
+        plan.append((anchor, arriving > 0, lands))
+    for phase in range(3):
+        for m, (anchor, arriving, lands) in enumerate(plan):
+            load = pltpu.make_async_copy(got_state.at[anchor], s_buf.at[m], in_s.at[m])
+            place = jnp.maximum(slots_ref[anchor, m, 2], 0)
+            store = pltpu.make_async_copy(s_buf.at[m], new_states.at[place], out_s.at[m])
+
+            @pl.when(arriving)
+            def _():
+                if phase == 0:
+                    load.start()
+                elif phase == 1:
+                    load.wait()
+                    store.start()
+                else:
+                    store.wait()
+
+            for j in range(per_request):
+                cload = pltpu.make_async_copy(
+                    got_cache.at[anchor, j], c_buf.at[m, j], in_c.at[m, j]
+                )
+                spot = jnp.maximum(blocks_ref[anchor, m, 1, j], 0)
+                cstore = pltpu.make_async_copy(
+                    c_buf.at[m, j], new_cache.at[spot], out_c.at[m, j]
+                )
+
+                @pl.when(lands[j])
+                def _():
+                    if phase == 0:
+                        cload.start()
+                    elif phase == 1:
+                        cload.wait()
+                        cstore.start()
+                    else:
+                        cstore.wait()
+
+
+def expert_kernel(
+    ranks, quads,
+    ids_ref, logits_ref, packed_ref, gate_ref, up_ref, down_ref, send_state, send_cache,
+    mixed_ref, got_state, got_cache,
+    g_buf, u_buf, d_buf, x_in, x_all, hidden, send_buf, recv_buf,
+    g_sem, u_sem, d_sem, own_sem, first_send, first_recv, second_send, second_recv,
+    back_send, back_recv, mig_send, mig_recv,
+):
+    d = lax.axis_index("dp")
+    e = lax.axis_index("ep")
+    devices = ranks * quads
+    me = d * quads + e
+    up_tiles = gate_ref.shape[2] // UP_TILE
+    down_tiles = down_ref.shape[2] // DOWN_TILE
+    ring = g_buf.shape[0]
+    experts = ranks
+
+    def up_copies(j, slot):
+        columns = pl.ds(pl.multiple_of(j * UP_TILE, UP_TILE), UP_TILE)
+        return (
+            pltpu.make_async_copy(gate_ref.at[0, :, columns], g_buf.at[slot], g_sem.at[slot]),
+            pltpu.make_async_copy(up_ref.at[0, :, columns], u_buf.at[slot], u_sem.at[slot]),
+        )
+
+    def down_copy(c):
+        columns = pl.ds(pl.multiple_of(c * DOWN_TILE, DOWN_TILE), DOWN_TILE)
+        return pltpu.make_async_copy(down_ref.at[0, :, columns], d_buf.at[c], d_sem.at[c])
+
+    for j in range(ring):
+        for copy in up_copies(j, j):
+            copy.start()
+
+    barrier = pltpu.get_barrier_semaphore()
+
+    @pl.loop(1, devices)
+    def _(k):
+        other = lax.rem(me + k, devices)
+        pl.semaphore_signal(
+            barrier, inc=1, device_id=(other // quads, lax.rem(other, quads)), device_id_type=MESH
+        )
+
+    pl.semaphore_wait(barrier, devices - 1)
+
+    own = pltpu.make_async_copy(packed_ref.at[d], x_in.at[me], own_sem)
+    own.start()
+    for k in range(1, ranks):
+        peer = lax.rem(d + k, ranks)
+        pltpu.make_async_remote_copy(
+            packed_ref.at[peer], x_in.at[me], first_send, first_recv.at[k],
+            device_id=(peer, e), device_id_type=MESH,
+        ).start()
+
+    def forward(src, slot):
+        for k in range(1, quads):
+            pltpu.make_async_remote_copy(
+                src, x_in.at[slot], second_send, second_recv,
+                device_id=(d, lax.rem(e + k, quads)), device_id_type=MESH,
+            ).start()
+
+    forward(packed_ref.at[d], me)
+
+    tok_count = logits_ref.shape[0]
+    picks, rows = target_rows(ids_ref, tok_count)
+    logits = logits_ref[...]
+    lane = lax.broadcasted_iota(jnp.int32, logits.shape, 1)
+    seat = lax.broadcasted_iota(jnp.int32, logits.shape, 0)
+    column = lax.broadcasted_iota(jnp.int32, (tok_count, devices * CAP), 1)
+    token = lax.broadcasted_iota(jnp.int32, (tok_count, devices * CAP), 0)
+    row_of = (column // (quads * CAP)) * CAP + lax.rem(column, CAP)
+    scores, hits = [], []
+    for k in range(2):
+        chosen = jnp.zeros(logits.shape, jnp.int32)
+        target = jnp.zeros(column.shape, jnp.int32)
+        for t in range(tok_count):
+            chosen = jnp.where(seat == t, picks[2 * t + k], chosen)
+            target = jnp.where(token == t, rows[2 * t + k], target)
+        value = jnp.sum(jnp.where(lane == chosen, logits, 0.0), axis=1, keepdims=True)
+        scores.append(jax.nn.sigmoid(value))
+        hits.append(row_of == target)
+    total = scores[0] + scores[1]
+    comb = jnp.where(hits[0], scores[0] / total, 0.0) + jnp.where(hits[1], scores[1] / total, 0.0)
+    comb_high = comb.astype(jnp.bfloat16)
+    comb_low = (comb - comb_high.astype(jnp.float32)).astype(jnp.bfloat16)
+
+    for k in range(1, ranks):
+        source = lax.rem(d - k + ranks, ranks)
+        slot = source * quads + e
+        pltpu.make_async_remote_copy(
+            x_in.at[slot], x_in.at[slot], first_send, first_recv.at[k],
+            device_id=(source, e), device_id_type=MESH,
+        ).wait_recv()
+        forward(x_in.at[slot], slot)
+    own.wait()
+    arrivals = ranks * (quads - 1)
+    pltpu.make_async_copy(
+        x_in.at[pl.ds(0, arrivals)], x_in.at[pl.ds(0, arrivals)], second_recv
+    ).wait()
+    for o in range(devices):
+        x_all[o * CAP : (o + 1) * CAP, :] = x_in[o]
+
+    for k in range(1, ranks):
+        peer = lax.rem(d + k, ranks)
+        for i, (src, dst) in enumerate(((send_state, got_state), (send_cache, got_cache))):
+            pltpu.make_async_remote_copy(
+                src.at[peer], dst.at[d], mig_send.at[i], mig_recv.at[i],
+                device_id=(peer, e), device_id_type=MESH,
+            ).start()
+
+    @pl.loop(0, up_tiles)
+    def _(j):
+        slot = lax.rem(j, ring)
+        for copy in up_copies(j, slot):
+            copy.wait()
+        gate = jnp.dot(x_all[...], g_buf[slot], preferred_element_type=jnp.float32)
+        upper = jnp.dot(x_all[...], u_buf[slot], preferred_element_type=jnp.float32)
+        value = gate / (1.0 + jnp.exp(-gate)) * upper
+        hidden[:, pl.ds(pl.multiple_of(j * UP_TILE, UP_TILE), UP_TILE)] = value.astype(jnp.bfloat16)
+
+        @pl.when(j < up_tiles - ring)
+        def _():
+            for copy in up_copies(j + ring, slot):
+                copy.start()
+
+        @pl.when(j < down_tiles)
+        def _():
+            down_copy(j).start()
+
+    @pl.loop(0, down_tiles)
+    def _(c):
+        down_copy(c).wait()
+        part = jnp.dot(hidden[...], d_buf[c], preferred_element_type=jnp.float32)
+        for o in range(devices):
+            send_buf[c, o] = part[o * CAP : (o + 1) * CAP].astype(jnp.bfloat16)
+        recv_buf[c, me] = send_buf[c, me]
+
+        @pl.loop(1, devices)
+        def _(k):
+            other = lax.rem(me + k, devices)
+            pltpu.make_async_remote_copy(
+                send_buf.at[c, other], recv_buf.at[c, me], back_send.at[c], back_recv.at[c],
+                device_id=(other // quads, lax.rem(other, quads)), device_id_type=MESH,
+            ).start()
+
+    @pl.loop(0, down_tiles)
+    def _(c):
+        most = recv_buf.at[c, pl.ds(0, devices - 1)]
+        pltpu.make_async_copy(most, most, back_recv.at[c]).wait()
+        rows_in = jnp.concatenate([recv_buf[c, o] for o in range(devices)], axis=0)
+        high = jnp.dot(comb_high, rows_in, preferred_element_type=jnp.float32)
+        low = jnp.dot(comb_low, rows_in, preferred_element_type=jnp.float32)
+        mixed_ref[:, pl.ds(pl.multiple_of(c * DOWN_TILE, DOWN_TILE), DOWN_TILE)] = (
+            high + low
+        ).astype(jnp.bfloat16)
+
+    for i, dst in enumerate((got_state, got_cache)):
+        most = dst.at[pl.ds(0, ranks - 1)]
+        pltpu.make_async_copy(most, most, mig_recv.at[i]).wait()
+        pltpu.make_async_copy(most, most, mig_send.at[i]).wait()
+    most = x_in.at[pl.ds(0, ranks - 1)]
+    pltpu.make_async_copy(most, most, first_send).wait()
+    most = x_in.at[pl.ds(0, arrivals)]
+    pltpu.make_async_copy(most, most, second_send).wait()
+
+    @pl.loop(0, down_tiles)
+    def _(c):
+        most = send_buf.at[c, pl.ds(0, devices - 1)]
+        pltpu.make_async_copy(most, most, back_send.at[c]).wait()
+
+
+def fused(
+    tokens, router, expert_ids, w_gate, w_up, w_down, states, kv_blocks,
+    plan_slots, plan_len, plan_blocks,
+):
+    ranks, quads = lax.axis_size("dp"), lax.axis_size("ep")
+    devices = ranks * quads
+    experts = router.shape[1]
+    tok_count, width = tokens.shape
+    moves = plan_slots.shape[1]
+    per_request = plan_blocks.shape[3]
+    bf16 = jnp.bfloat16
+    dma = pltpu.SemaphoreType.DMA
+    like = jax.ShapeDtypeStruct
+    state_one, cache_one = states.shape[1:], kv_blocks.shape[1:]
+    packed, send_state, send_cache, base_states, base_cache = pl.pallas_call(
+        prepare_kernel,
+        out_shape=(
+            like((experts, CAP, width), bf16),
+            like((ranks, *state_one), bf16),
+            like((ranks, per_request, *cache_one), bf16),
+            like(states.shape, bf16),
+            like(kv_blocks.shape, bf16),
+        ),
+        in_specs=[SMEM] * 4 + [VMEM, ANY, ANY],
+        out_specs=(VMEM, ANY, ANY, ANY, ANY),
+        scratch_shapes=[
+            pltpu.VMEM(states.shape, bf16),
+            pltpu.VMEM(kv_blocks.shape, bf16),
+            pltpu.VMEM((moves, *state_one), bf16),
+            pltpu.VMEM((moves, per_request, *cache_one), bf16),
+            dma((2,)), dma((moves,)), dma((moves, per_request)), dma((2,)),
+        ],
+        name="prepare",
+    )(expert_ids, plan_slots, plan_len, plan_blocks, tokens, states, kv_blocks)
+    logits = jnp.dot(tokens.astype(jnp.float32), router, precision=lax.Precision.HIGHEST)
+    depth = w_gate.shape[2]
+    ring = min(RING, depth // UP_TILE)
+    down_tiles = width // DOWN_TILE
+    mixed, got_state, got_cache = pl.pallas_call(
+        functools.partial(expert_kernel, ranks, quads),
+        out_shape=(
+            like((tok_count, width), bf16),
+            like((ranks, *state_one), bf16),
+            like((ranks, per_request, *cache_one), bf16),
+        ),
+        in_specs=[SMEM, VMEM, VMEM, ANY, ANY, ANY, ANY, ANY],
+        out_specs=(VMEM, ANY, ANY),
+        scratch_shapes=[
+            pltpu.VMEM((ring, width, UP_TILE), bf16),
+            pltpu.VMEM((ring, width, UP_TILE), bf16),
+            pltpu.VMEM((down_tiles, depth, DOWN_TILE), bf16),
+            pltpu.VMEM((devices, CAP, width), bf16),
+            pltpu.VMEM((devices * CAP, width), bf16),
+            pltpu.VMEM((devices * CAP, depth), bf16),
+            pltpu.VMEM((down_tiles, devices, CAP, DOWN_TILE), bf16),
+            pltpu.VMEM((down_tiles, devices, CAP, DOWN_TILE), bf16),
+            dma((ring,)), dma((ring,)), dma((down_tiles,)), dma,
+            dma, dma((ranks,)), dma, dma,
+            dma((down_tiles,)), dma((down_tiles,)), dma((2,)), dma((2,)),
+        ],
+        compiler_params=pltpu.CompilerParams(
+            collective_id=0, has_side_effects=True, vmem_limit_bytes=VMEM_LIMIT
+        ),
+        name="expert",
+    )(expert_ids, logits, packed, w_gate, w_up, w_down, send_state, send_cache)
+    new_states, new_cache = pl.pallas_call(
+        land_kernel,
+        out_shape=(like(states.shape, bf16), like(kv_blocks.shape, bf16)),
+        in_specs=[SMEM, SMEM, ANY, ANY, ANY, ANY],
+        out_specs=(ANY, ANY),
+        input_output_aliases={4: 0, 5: 1},
+        scratch_shapes=[
+            pltpu.VMEM((moves, *state_one), bf16),
+            pltpu.VMEM((moves, per_request, *cache_one), bf16),
+            dma((moves,)), dma((moves, per_request)), dma((moves,)), dma((moves, per_request)),
+        ],
+        name="land",
+    )(plan_slots, plan_blocks, got_state, got_cache, base_states, base_cache)
+    return mixed, new_states, new_cache
 
 
 def local(
@@ -126,8 +530,12 @@
         P(),
         P(),
     )
+    def step(*args):
+        one_slab = args[1].shape[1] == lax.axis_size("dp")
+        return (fused if one_slab else local)(*args)
+
     return jax.shard_map(
-        local,
+        step,
         mesh=mesh,
         in_specs=placed,
         out_specs=(P(("dp", "ep"), None), P("dp", None, "ep"), P("dp", None, None, "ep")),

time: 141 us -> 66.2 us (0.47)
  Pallas kernels: 0 us -> 56.5 us
  matrix products: 32.5 us -> 1.77 us
  starting transfers between devices: 24.9 us -> 0 us
  other arithmetic: 20.1 us -> 0 us
  waiting for transfers between devices: 18.3 us -> 0 us
  between operations: 18.2 us -> 0.66 us
  local copies, waits for them, and re-layouts: 18.9 us -> 6.81 us
  blocking collectives: 7.17 us -> 0 us
    pallas_call x0 -> x3, Pallas kernels: none -> 56.5 us  [the longest x1 49.3 us: fused(): pl.pallas_call(functools.partial(expert_kernel, ranks, quads), out_shape=...]
    dot_general x4 -> x1, matrix products: 32.5 us -> 1.77 us  [fused(): jnp.dot(tokens.astype(jnp.float32), router, precision=lax.Precision.HIGHEST)]
    all_to_all x4 -> x0, starting transfers between devices: 24.8 us -> none  [the longest x1 7.31 us: local(): lax.all_to_all(outgoing, 'dp', split_axis=0, concat_axis=0, tiled=True)]
    all_to_all x4 -> x0, waiting for transfers between devices: 18.1 us -> none  [the longest x1 11.3 us: local(): lax.all_to_all(send_state, 'dp', split_axis=0, concat_axis=0, tiled=True)]
    and x7 -> x0, other arithmetic: 9.68 us -> none  [the longest x4 6.06 us: local(): block_hit = (block_line == spot) & arriving[move_index]]
    gather x12 -> x0, local copies, waits for them, and re-layouts: 7.37 us -> none  [the longest x1 1.78 us: local(): state_out = states[jnp.maximum(leaving_slot, 0)]]
    all_gather x1 -> x0, blocking collectives: 7.17 us -> none  [local(): piece = lax.all_gather(rows_in, 'ep', axis=0, tiled=True)]
    unnamed x23 -> x5, local copies, waits for them, and re-layouts: 0.83 us -> 6.81 us
  transfers between devices with their start and end apart: 5 -> 0, of which waited for: 3 -> 0; matrix products, arithmetic and copies ran while one was open for 46% -> 0% of each run, Pallas kernels for 0% -> 0%
where the time goes in v1:
time: 66.2 us; the launch traced here: 65.7 us
  Pallas kernels  56.5 us (85%)
  local copies, waits for them, and re-layouts  6.81 us (10%)
  matrix products  1.77 us (3%)
    pallas_call x1, Pallas kernels, fused(): pl.pallas_call(functools.partial(expert_kernel, ranks, quads), out_shape=...  49.3 us
    unnamed x5, local copies, waits for them, and re-layouts  6.81 us
    pallas_call x1, Pallas kernels, fused(): pl.pallas_call(prepare_kernel, out_shape=(like((experts, CAP, width), bf1...  4.47 us
    pallas_call x1, Pallas kernels, fused(): pl.pallas_call(land_kernel, out_shape=(like(states.shape, bf16), like(kv_...  2.73 us
    dot_general x1, matrix products, fused(): jnp.dot(tokens.astype(jnp.float32), router, precision=lax.Precision.HIGHEST)  1.77 us

profile of v1, /device:TPU:0, one launch (start us, length us, event | category | flops | bytes accessed | tf_op | source)
XLA Modules:
  0.0 65.7 jit_solution(16521866641078103285)
XLA Ops:
  0.6 1.4 %copy.20.ids_ref = s32[4,2]{1,0:T(4,128)} copy(s32[4,2]{0,1:T(2,128)} %param.13) | data formatting | bytes 64 | tf_op args[2]
  2.0 1.8 %fusion.logits_ref = f32[4,8]{1,0:T(4,128)} fusion(bf16[4,4096]{1,0:T(4,128)(2,1)} %tok_ref.1, f32[4096,8]{0,1:T(8,128)} %param.12), kind=kOutput, calls=%fused_computation | convolution fusion | flops 1572864 | bytes 163968 | tf_op jit(solution)/shard_map/dot_general | solution.py:366
  3.8 1.4 %copy.17.slots_ref = s32[8,2,3]{2,1,0:T(2,128)} copy(s32[8,2,3]{0,1,2:T(2,128)} %param.19) | data formatting | bytes 384 | tf_op args[8]
  5.1 1.3 %copy.18.len_ref = s32[8,2]{1,0:T(8,128)} copy(s32[8,2]{0,1:T(2,128)} %param.20) | data formatting | bytes 128 | tf_op args[9]
  6.4 1.4 %copy.19.blocks_ref = s32[8,2,2,2]{3,2,1,0:T(2,128)} copy(s32[8,2,2,2]{0,3,2,1:T(2,128)} %param.21) | data formatting | bytes 512 | tf_op args[10]
  7.8 4.5 %prepare.1 = (bf16[8,2,4096]{2,1,0:T(2,128)(2,1)}, bf16[8,16,2048]{2,1,0:T(8,128)(2,1)}, bf16[8,2,2,16,256]{4,3,2,1,0:T(8,128)(2,1)}, bf16[16,16,2048]{2,1,0:T(8,128)(2,1)}, bf16[32,2,16,256]{3,2,1,0:T(8,128)(2,1)}) custom-call(s32[4,2]{1,0:T(4,128)} %copy.20.ids_ref, s32[8,2,3]{2,1,0:T(2,128)} %copy.17.slots_ref, s32[8,2]{1,0:T(8,128)} %copy.18.len_ref, ...), custom_call_target="tpu_custom_call" | custom-call | tf_op jit(solution)/shard_map/prepare/pallas_call | solution.py:346
  12.3 49.3 %expert.1 = (bf16[4,4096]{1,0:T(4,128)(2,1)}, bf16[8,16,2048]{2,1,0:T(8,128)(2,1)}, bf16[8,2,2,16,256]{4,3,2,1,0:T(8,128)(2,1)}) custom-call(s32[4,2]{1,0:T(4,128)} %copy.20.ids_ref, f32[4,8]{1,0:T(4,128)} %fusion.logits_ref, bf16[8,2,4096]{2,1,0:T(2,128)(2,1)} %get-tuple-element.13.packed_ref, bf16[1,4096,3072]{2,1,0:T(8,128)(2,1)} %gate_ref.1, ...), custom_call_target="tpu_custom_call" | custom-call | tf_op jit(solution)/shard_map/expert/pallas_call | solution.py:370
  61.6 2.7 %land.1 = (bf16[16,16,2048]{2,1,0:T(8,128)(2,1)}, bf16[32,2,16,256]{3,2,1,0:T(8,128)(2,1)}) custom-call(s32[8,2,3]{2,1,0:T(2,128)} %copy.17.slots_ref, s32[8,2,2,2]{3,2,1,0:T(2,128)} %copy.19.blocks_ref, bf16[8,16,2048]{2,1,0:T(8,128)(2,1)} %get-tuple-element.17.got_state, ...), custom_call_target="tpu_custom_call", output_to_operand_aliasing={{0}: (4, {}), {1}: (5, {})} | custom-call | tf_op jit(solution)/shard_map/land/pallas_call | solution.py:397
  64.3 1.4 %copy.26 = bf16[4,4096]{1,0:T(4,128)(2,1)} copy(bf16[4,4096]{1,0:T(4,128)(2,1)} %get-tuple-element.26) | data formatting | bytes 65536

commit v2 on v1

--- a/solution.py
+++ b/solution.py
@@ -19,7 +19,7 @@
 
 
 def target_rows(ids_ref, tok_count):
-    picks = [ids_ref[t, k] for t in range(tok_count) for k in range(2)]
+    picks = [ids_ref[k, t] for t in range(tok_count) for k in range(2)]
     rows = []
     for p, expert in enumerate(picks):
         slot = jnp.int32(0)
@@ -29,141 +29,83 @@
     return picks, rows
 
 
-def prepare_kernel(
-    ids_ref, slots_ref, len_ref, blocks_ref, tok_ref, states_ref, kv_ref,
-    packed_ref, send_state, send_cache, base_states, base_cache,
-    s_buf, c_buf, s_pay, c_pay, load_sem, pay_sem, cpay_sem, store_sem,
+def land_kernel(
+    slots_ref, blocks_ref, got_state, got_cache, states_ref, kv_ref, part_ref,
+    new_states, new_cache, mixed_ref, s_all, c_all, m_all, s_buf, c_buf,
+    in_sem, in_s, in_c, out_sem,
 ):
     here = lax.axis_index("dp")
-    moves = slots_ref.shape[1]
-    per_request = blocks_ref.shape[3]
-    block_len = kv_ref.shape[2]
-    load_s = pltpu.make_async_copy(states_ref, s_buf, load_sem.at[0])
-    load_c = pltpu.make_async_copy(kv_ref, c_buf, load_sem.at[1])
-    load_s.start()
-    load_c.start()
-    tok_count = tok_ref.shape[0]
-    experts = packed_ref.shape[0]
-    _, rows = target_rows(ids_ref, tok_count)
-    row_at = lax.broadcasted_iota(jnp.int32, (experts * CAP, tok_count), 0)
-    tok_at = lax.broadcasted_iota(jnp.int32, (experts * CAP, tok_count), 1)
-    placer = jnp.zeros((experts * CAP, tok_count), jnp.float32)
-    for p, row in enumerate(rows):
-        placer = jnp.where((row_at == row) & (tok_at == p // 2), 1.0, placer)
-    packed = jnp.dot(
-        placer.astype(jnp.bfloat16), tok_ref[...], preferred_element_type=jnp.float32
-    ).astype(jnp.bfloat16)
-    for e in range(experts):
-        packed_ref[e] = packed[e * CAP : (e + 1) * CAP]
-    load_s.wait()
-    load_c.wait()
-    for m in range(moves):
-        slot = slots_ref[here, m, 0]
-        dest = slots_ref[here, m, 1]
-
-        @pl.when(slot >= 0)
-        def _():
-            s_pay[m] = s_buf[slot]
-            s_buf[slot] = jnp.zeros_like(s_pay[m])
-            pltpu.make_async_copy(s_pay.at[m], send_state.at[dest], pay_sem.at[m]).start()
-
-        for j in range(per_request):
-            block = blocks_ref[here, m, 0, j]
-
-            @pl.when(block >= 0)
-            def _():
-                value = c_buf[block]
-                position = j * block_len + lax.broadcasted_iota(jnp.int32, value.shape, 1)
-                c_pay[m, j] = jnp.where(
-                    position < len_ref[here, m], value.astype(jnp.float32), 0.0
-                ).astype(value.dtype)
-                c_buf[block] = jnp.zeros_like(value)
-                pltpu.make_async_copy(
-                    c_pay.at[m, j], send_cache.at[dest, j], cpay_sem.at[m, j]
-                ).start()
-
-    store_s = pltpu.make_async_copy(s_buf, base_states, store_sem.at[0])
-    store_c = pltpu.make_async_copy(c_buf, base_cache, store_sem.at[1])
-    store_s.start()
-    store_c.start()
-    for m in range(moves):
-        slot = slots_ref[here, m, 0]
-        dest = slots_ref[here, m, 1]
-
-        @pl.when(slot >= 0)
-        def _():
-            pltpu.make_async_copy(s_pay.at[m], send_state.at[dest], pay_sem.at[m]).wait()
-
-        for j in range(per_request):
-
-            @pl.when(blocks_ref[here, m, 0, j] >= 0)
-            def _():
-                pltpu.make_async_copy(
-                    c_pay.at[m, j], send_cache.at[dest, j], cpay_sem.at[m, j]
-                ).wait()
-
-    store_s.wait()
-    store_c.wait()
-
-
-def land_kernel(
-    slots_ref, blocks_ref, got_state, got_cache, base_states, base_cache,
-    new_states, new_cache, s_buf, c_buf, in_s, in_c, out_s, out_c,
-):
-    here = lax.axis_index("dp")
-    ranks, moves = slots_ref.shape[0], slots_ref.shape[1]
-    per_request = blocks_ref.shape[3]
+    moves, ranks = slots_ref.shape[1:]
+    per_request = blocks_ref.shape[2]
+    whole = ((states_ref, s_all, new_states), (kv_ref, c_all, new_cache), (part_ref, m_all, mixed_ref))
+    loads = [pltpu.make_async_copy(a, b, in_sem.at[i]) for i, (a, b, _) in enumerate(whole)]
+    stores = [pltpu.make_async_copy(b, c, out_sem.at[i]) for i, (_, b, c) in enumerate(whole)]
+    for copy in loads:
+        copy.start()
     plan = []
     for m in range(moves):
         anchor, arriving = jnp.int32(0), jnp.int32(0)
         for r in range(ranks):
-            hit = slots_ref[r, m, 1] == here
+            hit = slots_ref[1, m, r] == here
             anchor = jnp.where(hit, r, anchor)
             arriving = jnp.where(hit, 1, arriving)
-        lands = [
-            (arriving > 0) & (blocks_ref[anchor, m, 1, j] >= 0) for j in range(per_request)
-        ]
-        plan.append((anchor, arriving > 0, lands))
-    for phase in range(3):
-        for m, (anchor, arriving, lands) in enumerate(plan):
-            load = pltpu.make_async_copy(got_state.at[anchor], s_buf.at[m], in_s.at[m])
-            place = jnp.maximum(slots_ref[anchor, m, 2], 0)
-            store = pltpu.make_async_copy(s_buf.at[m], new_states.at[place], out_s.at[m])
-
-            @pl.when(arriving)
+        plan.append((anchor, arriving > 0))
+
+    def state_load(m, anchor):
+        return pltpu.make_async_copy(got_state.at[anchor], s_buf.at[m], in_s.at[m])
+
+    def cache_load(m, j, anchor):
+        return pltpu.make_async_copy(got_cache.at[anchor, j], c_buf.at[m, j], in_c.at[m, j])
+
+    for m, (anchor, arriving) in enumerate(plan):
+
+        @pl.when(arriving)
+        def _():
+            state_load(m, anchor).start()
+            for j in range(per_request):
+                cache_load(m, j, anchor).start()
+
+    for copy in loads:
+        copy.wait()
+    stores[2].start()
+    for m, (anchor, arriving) in enumerate(plan):
+        slot = slots_ref[0, m, here]
+
+        @pl.when(slot >= 0)
+        def _():
+            s_all[slot] = jnp.zeros_like(s_buf[m])
+
+        for j in range(per_request):
+            block = blocks_ref[m, 0, j, here]
+
+            @pl.when(block >= 0)
             def _():
-                if phase == 0:
-                    load.start()
-                elif phase == 1:
-                    load.wait()
-                    store.start()
-                else:
-                    store.wait()
-
+                c_all[block] = jnp.zeros_like(c_buf[m, j])
+
+        @pl.when(arriving)
+        def _():
+            state_load(m, anchor).wait()
+            s_all[slots_ref[2, m, anchor]] = s_buf[m]
             for j in range(per_request):
-                cload = pltpu.make_async_copy(
-                    got_cache.at[anchor, j], c_buf.at[m, j], in_c.at[m, j]
-                )
-                spot = jnp.maximum(blocks_ref[anchor, m, 1, j], 0)
-                cstore = pltpu.make_async_copy(
-                    c_buf.at[m, j], new_cache.at[spot], out_c.at[m, j]
-                )
-
-                @pl.when(lands[j])
+                cache_load(m, j, anchor).wait()
+                spot = blocks_ref[m, 1, j, anchor]
+
+                @pl.when(spot >= 0)
                 def _():
-                    if phase == 0:
-                        cload.start()
-                    elif phase == 1:
-                        cload.wait()
-                        cstore.start()
-                    else:
-                        cstore.wait()
+                    c_all[spot] = c_buf[m, j]
+
+    stores[0].start()
+    stores[1].start()
+    for copy in stores:
+        copy.wait()
 
 
 def expert_kernel(
     ranks, quads,
-    ids_ref, logits_ref, packed_ref, gate_ref, up_ref, down_ref, send_state, send_cache,
+    ids_ref, slots_ref, len_ref, blocks_ref, tok_ref, router_ref, gate_ref, up_ref, down_ref,
+    states_ref, kv_ref,
     mixed_ref, got_state, got_cache,
+    packed_ref, s_all, c_all, s_pay, c_pay, send_state, send_cache, mig_load,
     g_buf, u_buf, d_buf, x_in, x_all, hidden, send_buf, recv_buf,
     g_sem, u_sem, d_sem, own_sem, first_send, first_recv, second_send, second_recv,
     back_send, back_recv, mig_send, mig_recv,
@@ -192,6 +134,13 @@
         for copy in up_copies(j, j):
             copy.start()
 
+    load_states = pltpu.make_async_copy(states_ref, s_all, mig_load.at[0])
+    load_cache = pltpu.make_async_copy(kv_ref, c_all, mig_load.at[1])
+    load_states.start()
+    load_cache.start()
+    for c in range(down_tiles):
+        down_copy(c).start()
+
     barrier = pltpu.get_barrier_semaphore()
 
     @pl.loop(1, devices)
@@ -200,6 +149,19 @@
         pl.semaphore_signal(
             barrier, inc=1, device_id=(other // quads, lax.rem(other, quads)), device_id_type=MESH
         )
+
+    tok_count = tok_ref.shape[0]
+    picks, rows = target_rows(ids_ref, tok_count)
+    row_at = lax.broadcasted_iota(jnp.int32, (experts * CAP, tok_count), 0)
+    tok_at = lax.broadcasted_iota(jnp.int32, (experts * CAP, tok_count), 1)
+    placer = jnp.zeros((experts * CAP, tok_count), jnp.float32)
+    for p, row in enumerate(rows):
+        placer = jnp.where((row_at == row) & (tok_at == p // 2), 1.0, placer)
+    packed = jnp.dot(
+        placer.astype(jnp.bfloat16), tok_ref[...], preferred_element_type=jnp.float32
+    ).astype(jnp.bfloat16)
+    for r in range(experts):
+        packed_ref[r] = packed[r * CAP : (r + 1) * CAP]
 
     pl.semaphore_wait(barrier, devices - 1)
 
@@ -221,11 +183,13 @@
 
     forward(packed_ref.at[d], me)
 
-    tok_count = logits_ref.shape[0]
-    picks, rows = target_rows(ids_ref, tok_count)
-    logits = logits_ref[...]
-    lane = lax.broadcasted_iota(jnp.int32, logits.shape, 1)
-    seat = lax.broadcasted_iota(jnp.int32, logits.shape, 0)
+    wide = tok_ref[...].astype(jnp.float32)
+    lane = lax.broadcasted_iota(jnp.int32, (tok_count, experts), 1)
+    seat = lax.broadcasted_iota(jnp.int32, (tok_count, experts), 0)
+    logits = jnp.zeros((tok_count, experts), jnp.float32)
+    for r in range(experts):
+        product = jnp.sum(wide * router_ref[r : r + 1, :], axis=1, keepdims=True)
+        logits = jnp.where(lane == r, product, logits)
     column = lax.broadcasted_iota(jnp.int32, (tok_count, devices * CAP), 1)
     token = lax.broadcasted_iota(jnp.int32, (tok_count, devices * CAP), 0)
     row_of = (column // (quads * CAP)) * CAP + lax.rem(column, CAP)
@@ -252,6 +216,41 @@
             device_id=(source, e), device_id_type=MESH,
         ).wait_recv()
         forward(x_in.at[slot], slot)
+
+    load_states.wait()
+    load_cache.wait()
+    moves = slots_ref.shape[1]
+    per_request = blocks_ref.shape[2]
+    block_len = kv_ref.shape[2]
+    position = lax.broadcasted_iota(jnp.int32, kv_ref.shape[1:], 1)
+    for m in range(moves):
+        slot = slots_ref[0, m, d]
+        s_pay[m] = jnp.zeros_like(s_pay[m])
+
+        @pl.loop(0, s_all.shape[0])
+        def _(s):
+            s_pay[m] = lax.select(slot == s, s_all[s], s_pay[m])
+
+        for j in range(per_request):
+            block = blocks_ref[m, 0, j, d]
+            c_pay[m, j] = jnp.zeros_like(c_pay[m, j])
+
+            @pl.loop(0, c_all.shape[0])
+            def _(s):
+                c_pay[m, j] = lax.select(block == s, c_all[s], c_pay[m, j])
+
+            kept = c_pay[m, j].astype(jnp.float32)
+            kept = jnp.where(j * block_len + position < len_ref[m, d], kept, 0.0)
+            c_pay[m, j] = kept.astype(jnp.bfloat16)
+    for r in range(ranks):
+        s_value, c_value = s_pay[0], c_pay[0]
+        for m in range(1, moves):
+            hit = slots_ref[1, m, d] == r
+            s_value = lax.select(hit, s_pay[m], s_value)
+            c_value = lax.select(hit, c_pay[m], c_value)
+        send_state[r] = s_value
+        send_cache[r] = c_value
+
     own.wait()
     arrivals = ranks * (quads - 1)
     pltpu.make_async_copy(
@@ -282,10 +281,6 @@
         def _():
             for copy in up_copies(j + ring, slot):
                 copy.start()
-
-        @pl.when(j < down_tiles)
-        def _():
-            down_copy(j).start()
 
     @pl.loop(0, down_tiles)
     def _(c):
@@ -343,27 +338,10 @@
     dma = pltpu.SemaphoreType.DMA
     like = jax.ShapeDtypeStruct
     state_one, cache_one = states.shape[1:], kv_blocks.shape[1:]
-    packed, send_state, send_cache, base_states, base_cache = pl.pallas_call(
-        prepare_kernel,
-        out_shape=(
-            like((experts, CAP, width), bf16),
-            like((ranks, *state_one), bf16),
-            like((ranks, per_request, *cache_one), bf16),
-            like(states.shape, bf16),
-            like(kv_blocks.shape, bf16),
-        ),
-        in_specs=[SMEM] * 4 + [VMEM, ANY, ANY],
-        out_specs=(VMEM, ANY, ANY, ANY, ANY),
-        scratch_shapes=[
-            pltpu.VMEM(states.shape, bf16),
-            pltpu.VMEM(kv_blocks.shape, bf16),
-            pltpu.VMEM((moves, *state_one), bf16),
-            pltpu.VMEM((moves, per_request, *cache_one), bf16),
-            dma((2,)), dma((moves,)), dma((moves, per_request)), dma((2,)),
-        ],
-        name="prepare",
-    )(expert_ids, plan_slots, plan_len, plan_blocks, tokens, states, kv_blocks)
-    logits = jnp.dot(tokens.astype(jnp.float32), router, precision=lax.Precision.HIGHEST)
+    ids = expert_ids.T
+    slots = jnp.transpose(plan_slots, (2, 1, 0))
+    lengths = plan_len.T
+    blocks = jnp.transpose(plan_blocks, (1, 2, 3, 0))
     depth = w_gate.shape[2]
     ring = min(RING, depth // UP_TILE)
     down_tiles = width // DOWN_TILE
@@ -374,9 +352,17 @@
             like((ranks, *state_one), bf16),
             like((ranks, per_request, *cache_one), bf16),
         ),
-        in_specs=[SMEM, VMEM, VMEM, ANY, ANY, ANY, ANY, ANY],
+        in_specs=[SMEM] * 4 + [VMEM] * 2 + [ANY] * 5,
         out_specs=(VMEM, ANY, ANY),
         scratch_shapes=[
+            pltpu.VMEM((experts, CAP, width), bf16),
+            pltpu.VMEM(states.shape, bf16),
+            pltpu.VMEM(kv_blocks.shape, bf16),
+            pltpu.VMEM((moves, *state_one), bf16),
+            pltpu.VMEM((moves, per_request, *cache_one), bf16),
+            pltpu.VMEM((ranks, *state_one), bf16),
+            pltpu.VMEM((ranks, per_request, *cache_one), bf16),
+            dma((2,)),
             pltpu.VMEM((ring, width, UP_TILE), bf16),
             pltpu.VMEM((ring, width, UP_TILE), bf16),
             pltpu.VMEM((down_tiles, depth, DOWN_TILE), bf16),
@@ -393,20 +379,24 @@
             collective_id=0, has_side_effects=True, vmem_limit_bytes=VMEM_LIMIT
         ),
         name="expert",
-    )(expert_ids, logits, packed, w_gate, w_up, w_down, send_state, send_cache)
-    new_states, new_cache = pl.pallas_call(
+    )(
+        ids, slots, lengths, blocks, tokens, router.T, w_gate, w_up, w_down, states, kv_blocks
+    )
+    new_states, new_cache, mixed = pl.pallas_call(
         land_kernel,
-        out_shape=(like(states.shape, bf16), like(kv_blocks.shape, bf16)),
-        in_specs=[SMEM, SMEM, ANY, ANY, ANY, ANY],
-        out_specs=(ANY, ANY),
-        input_output_aliases={4: 0, 5: 1},
+        out_shape=(like(states.shape, bf16), like(kv_blocks.shape, bf16), like(mixed.shape, bf16)),
+        in_specs=[SMEM, SMEM] + [ANY] * 5,
+        out_specs=(ANY, ANY, ANY),
         scratch_shapes=[
+            pltpu.VMEM(states.shape, bf16),
+            pltpu.VMEM(kv_blocks.shape, bf16),
+            pltpu.VMEM(mixed.shape, bf16),
             pltpu.VMEM((moves, *state_one), bf16),
             pltpu.VMEM((moves, per_request, *cache_one), bf16),
-            dma((moves,)), dma((moves, per_request)), dma((moves,)), dma((moves, per_request)),
+            dma((3,)), dma((moves,)), dma((moves, per_request)), dma((3,)),
         ],
         name="land",
-    )(plan_slots, plan_blocks, got_state, got_cache, base_states, base_cache)
+    )(slots, blocks, got_state, got_cache, states, kv_blocks, mixed)
     return mixed, new_states, new_cache
 
 

time: 66.2 us -> 60.6 us (0.915)
  local copies, waits for them, and re-layouts: 6.81 us -> 0 us
  Pallas kernels: 56.5 us -> 59.8 us
  matrix products: 1.77 us -> 0 us
    pallas_call x1, Pallas kernels: 49.3 us -> 56.3 us  [fused(): pl.pallas_call(functools.partial(expert_kernel, ranks, quads), out_shape=...]
    unnamed x5 -> x0, local copies, waits for them, and re-layouts: 6.81 us -> none
    pallas_call x1 -> x0, Pallas kernels: 4.47 us -> none  [fused(): pl.pallas_call(prepare_kernel, out_shape=(like((experts, CAP, width), bf1...]
    dot_general x1 -> x0, matrix products: 1.77 us -> none  [fused(): jnp.dot(tokens.astype(jnp.float32), router, precision=lax.Precision.HIGHEST)]
    pallas_call x1, Pallas kernels: 2.73 us -> 3.51 us  [fused(): pl.pallas_call(land_kernel, out_shape=(like(states.shape, bf16), like(kv_...]
where the time goes in v2:
time: 60.6 us; the launch traced here: 60.4 us
  Pallas kernels  59.8 us (99%)
  between operations  0.64 us (1%)
    pallas_call x1, Pallas kernels, fused(): pl.pallas_call(functools.partial(expert_kernel, ranks, quads), out_shape=...  56.3 us
    pallas_call x1, Pallas kernels, fused(): pl.pallas_call(land_kernel, out_shape=(like(states.shape, bf16), like(kv_...  3.51 us

profile of v2, /device:TPU:0, one launch (start us, length us, event | category | flops | bytes accessed | tf_op | source)
XLA Modules:
  0.0 60.4 jit_solution(16269971911948183970)
XLA Ops:
  0.6 56.3 %expert.1 = (bf16[4,4096]{1,0:T(4,128)(2,1)}, bf16[8,16,2048]{2,1,0:T(8,128)(2,1)}, bf16[8,2,2,16,256]{4,3,2,1,0:T(8,128)(2,1)}) custom-call(s32[2,4]{1,0:T(2,128)} %bitcast.10, s32[3,2,8]{2,1,0:T(2,128)} %bitcast.8, s32[2,8]{1,0:T(2,128)} %bitcast.11, s32[2,2,2,8]{3,2,1,0:T(2,128)} %bitcast.6, bf16[4,4096]{1,0:T(4,128)(2,1)} %tok_ref.1, f32[8,4096]{1,0:T(8,128)} %bitcast.5, ...), custom_call_target="tpu_custom_call" | custom-call | tf_op jit(solution)/shard_map/expert/pallas_call | solution.py:348
  56.9 3.5 %land.1 = (bf16[16,16,2048]{2,1,0:T(8,128)(2,1)}, bf16[32,2,16,256]{3,2,1,0:T(8,128)(2,1)}, bf16[4,4096]{1,0:T(4,128)(2,1)}) custom-call(s32[3,2,8]{2,1,0:T(2,128)} %bitcast.9, s32[2,2,2,8]{3,2,1,0:T(2,128)} %bitcast.7, bf16[8,16,2048]{2,1,0:T(8,128)(2,1)} %get-tuple-element.9.got_state, bf16[8,2,2,16,256]{4,3,2,1,0:T(8,128)(2,1)} %get-tuple-element.10.got_cache, ...), custom_call_target="tpu_custom_call" | custom-call | tf_op jit(solution)/shard_map/land/pallas_call | solution.py:385

commit v3 on v2

--- a/solution.py
+++ b/solution.py
@@ -130,14 +130,14 @@
         columns = pl.ds(pl.multiple_of(c * DOWN_TILE, DOWN_TILE), DOWN_TILE)
         return pltpu.make_async_copy(down_ref.at[0, :, columns], d_buf.at[c], d_sem.at[c])
 
-    for j in range(ring):
-        for copy in up_copies(j, j):
-            copy.start()
-
     load_states = pltpu.make_async_copy(states_ref, s_all, mig_load.at[0])
     load_cache = pltpu.make_async_copy(kv_ref, c_all, mig_load.at[1])
     load_states.start()
     load_cache.start()
+    for j in range(ring):
+        for copy in up_copies(j, j):
+            copy.start()
+
     for c in range(down_tiles):
         down_copy(c).start()
 

time: 60.6 us -> 59.4 us (0.980)
  Pallas kernels: 59.8 us -> 58.5 us
    pallas_call x1, Pallas kernels: 56.3 us -> 55 us  [fused(): pl.pallas_call(functools.partial(expert_kernel, ranks, quads), out_shape=...]
where the time goes in v3:
time: 59.4 us; the launch traced here: 59.2 us
  Pallas kernels  58.5 us (98%)
  between operations  0.64 us (1%)
    pallas_call x1, Pallas kernels, fused(): pl.pallas_call(functools.partial(expert_kernel, ranks, quads), out_shape=...  55 us
    pallas_call x1, Pallas kernels, fused(): pl.pallas_call(land_kernel, out_shape=(like(states.shape, bf16), like(kv_...  3.51 us

profile of v3, /device:TPU:0, one launch (start us, length us, event | category | flops | bytes accessed | tf_op | source)
XLA Modules:
  0.0 59.2 jit_solution(18275584761322940690)
XLA Ops:
  0.6 55.0 %expert.1 = (bf16[4,4096]{1,0:T(4,128)(2,1)}, bf16[8,16,2048]{2,1,0:T(8,128)(2,1)}, bf16[8,2,2,16,256]{4,3,2,1,0:T(8,128)(2,1)}) custom-call(s32[2,4]{1,0:T(2,128)} %bitcast.10, s32[3,2,8]{2,1,0:T(2,128)} %bitcast.8, s32[2,8]{1,0:T(2,128)} %bitcast.11, s32[2,2,2,8]{3,2,1,0:T(2,128)} %bitcast.6, bf16[4,4096]{1,0:T(4,128)(2,1)} %tok_ref.1, f32[8,4096]{1,0:T(8,128)} %bitcast.5, ...), custom_call_target="tpu_custom_call" | custom-call | tf_op jit(solution)/shard_map/expert/pallas_call | solution.py:348
  55.7 3.5 %land.1 = (bf16[16,16,2048]{2,1,0:T(8,128)(2,1)}, bf16[32,2,16,256]{3,2,1,0:T(8,128)(2,1)}, bf16[4,4096]{1,0:T(4,128)(2,1)}) custom-call(s32[3,2,8]{2,1,0:T(2,128)} %bitcast.9, s32[2,2,2,8]{3,2,1,0:T(2,128)} %bitcast.7, bf16[8,16,2048]{2,1,0:T(8,128)(2,1)} %get-tuple-element.9.got_state, bf16[8,2,2,16,256]{4,3,2,1,0:T(8,128)(2,1)} %get-tuple-element.10.got_cache, ...), custom_call_target="tpu_custom_call" | custom-call | tf_op jit(solution)/shard_map/land/pallas_call | solution.py:385
